TPU v7x, 32 devices: a whole 2x2x4 slice. The times are simulated.
32 devices in a mesh: lat: 8 (over y, x, core), rad: 4 (over z).
Axes of the slice: x: 2, y: 2, z: 4, core: 2. Of those that a mesh axis runs over, the one named last changes fastest.
Arguments:
- schur_off: bfloat16 [8, 4, 1536, 1536], P('lat', 'rad'), may hold values from -0.15625 to 0.15625
- schur_diag: float32 [8, 4, 1536], P('lat', 'rad'), may hold values from 1.5 to 4
- source: float32 [8, 4, 1536, 128], P('lat', 'rad'), may hold values from -6 to 6
- start: float32 [8, 4, 1536, 128], P('lat', 'rad'), may hold values from -6 to 6
- decay: float32 [8, 4, 256, 128], P('lat', 'rad'), may hold values from 0.2 to 1
- neighbour_face: int32 [8, 4], replicated, may hold values from 0 to 3
- orientation: int32 [8, 4], replicated, may hold values from 0 to 7
Outputs:
- traces: float32 [8, 4, 1536, 128], P('lat', 'rad')
Inputs may be any that keep to these rules, and one draw needn't show every extreme that they name: `neighbour_face`: a face index of 0 to 3. `orientation`: a code of 0 to 7 whose bits select transpose, row reflection and column reflection.
All inputs are finite; a program needn't handle non-finite values.
Results may differ from a plain program's by a relative error of at most 0.001.
Values sent between devices are 32-bit elements; how exact they have to be, the bound alone decides.
A program may use at most 64 MiB of HBM per device.

v0:
```python
import functools
import math

import jax
import jax.numpy as jnp
from jax import lax
from jax.experimental import pallas as pl
from jax.experimental.pallas import tpu as pltpu
from jax.sharding import PartitionSpec as P

ITERS = 2
RADIAL_PASSES = 2
OMEGA = 0.3
COUPLE = 0.5
CHUNKS = 8
SEND_ORDER = (2, 3, 0, 1)
MESH = pl.DeviceIdType.MESH


def permuted(face, code, side):
    nodes = side * side
    n = lax.broadcasted_iota(jnp.int32, (nodes, 1), 0)
    i, j = n // side, n % side
    swap, rows, cols = code & 1, (code >> 1) & 1, (code >> 2) & 1
    a = i + swap * (j - i)
    b = j + swap * (i - j)
    a = a + rows * (side - 1 - 2 * a)
    b = b + cols * (side - 1 - 2 * b)
    at = lax.broadcasted_iota(jnp.int32, (nodes, nodes), 1)
    hot = jnp.where(at == a * side + b, 1.0, 0.0).astype(jnp.bfloat16)
    high = face.astype(jnp.bfloat16)
    rest = face - high.astype(jnp.float32)
    middle = rest.astype(jnp.bfloat16)
    low = (rest - middle.astype(jnp.float32)).astype(jnp.bfloat16)
    total = None
    for part in (low, middle, high):
        moved = jnp.dot(hot, part, preferred_element_type=jnp.float32)
        total = moved if total is None else total + moved
    return total


def kernel(
    lat_count, rad_count, nodes,
    face_at, code_at, diag_ref, w_hbm, source_hbm, start_hbm, decay_hbm,
    out_ref,
    w, ub, rhs, factor, diag, res, ready,
    lat_out, lat_in, dn_out, dn_in, h_out, h_in,
    load_sem, w_sem,
    lat_send, lat_recv, dn_send, dn_recv, h_send, h_recv,
):
    side = math.isqrt(nodes)
    far = max(2, lat_count // 8)
    offsets = (-1, 1, -far, far)
    p = lax.axis_index("lat")
    r = lax.axis_index("rad")
    size = nodes // CHUNKS
    u = out_ref.at[0, 0]
    lanes = u.shape[1]
    upper, lower = slice(0, 4 * nodes), slice(4 * nodes, 6 * nodes)

    load_u = pltpu.make_async_copy(start_hbm.at[0, 0], u, load_sem.at[0])
    load_rhs = pltpu.make_async_copy(source_hbm.at[0, 0], rhs, load_sem.at[1])
    load_factor = pltpu.make_async_copy(decay_hbm.at[0, 0], factor, load_sem.at[2])
    load_w = [
        pltpu.make_async_copy(w_hbm.at[0, 0, part], w.at[part], w_sem.at[n])
        for n, part in enumerate((upper, lower))
    ]
    load_u.start()
    for copy in load_w:
        copy.start()
    load_rhs.start()
    load_factor.start()

    barrier = pltpu.get_barrier_semaphore()
    for offset in offsets:
        target = (p - offset + lat_count) % lat_count
        pl.semaphore_signal(barrier, inc=1, device_id={"lat": target}, device_id_type=MESH)

    below, above = (r - 1 + rad_count) % rad_count, (r + 1) % rad_count

    @pl.when(r > 0)
    def _():
        pl.semaphore_signal(barrier, inc=1, device_id={"rad": below}, device_id_type=MESH)

    @pl.when(r < rad_count - 1)
    def _():
        pl.semaphore_signal(barrier, inc=1, device_id={"rad": above}, device_id_type=MESH)

    inner = (r + rad_count - 1) // rad_count + (2 * rad_count - 2 - r) // rad_count

    def lat_copy(outer, k):
        target = (p - offsets[k] + lat_count) % lat_count
        return pltpu.make_async_remote_copy(
            src_ref=lat_out.at[outer, k], dst_ref=lat_in.at[outer, k],
            send_sem=lat_send.at[outer, k], recv_sem=lat_recv.at[outer, k],
            device_id={"lat": target}, device_id_type=MESH,
        )

    def dn_copy(sweep):
        return pltpu.make_async_remote_copy(
            src_ref=dn_out.at[sweep], dst_ref=dn_in.at[sweep],
            send_sem=dn_send.at[sweep], recv_sem=dn_recv.at[sweep],
            device_id={"rad": below}, device_id_type=MESH,
        )

    def h_copy(sweep, c):
        rows = pl.ds(c * size, size)
        return pltpu.make_async_remote_copy(
            src_ref=h_out.at[sweep, rows], dst_ref=h_in.at[sweep, rows],
            send_sem=h_send.at[sweep, c], recv_sem=h_recv.at[sweep, c],
            device_id={"rad": above}, device_id_type=MESH,
        )

    def make_faces(outer, which_faces):
        for k in which_faces:
            target = (p - offsets[k] + lat_count) % lat_count
            which = jnp.full((nodes, lanes), face_at[k, target], jnp.int32)
            face = u[slice(0, nodes), :]
            for f in range(1, 4):
                face = jnp.where(which == f, u[slice(f * nodes, (f + 1) * nodes), :], face)
            lat_out[outer, k] = permuted(face, code_at[k, target], side)

    def start_faces(outer, which_faces):
        for k in which_faces:
            lat_copy(outer, k).start()

    def residual(part):
        applied = jnp.dot(w[part, :], ub[...], preferred_element_type=jnp.float32)
        return rhs[part, :] - (applied + diag[part, :] * u[part, :])

    load_u.wait()
    make_faces(0, SEND_ORDER[:2])
    pl.semaphore_wait(barrier, len(offsets) + inner)
    start_faces(0, SEND_ORDER[:2])
    for k in SEND_ORDER[2:]:
        make_faces(0, (k,))
        start_faces(0, (k,))
    ub[...] = u[...].astype(jnp.bfloat16)
    for block in range(6 * nodes // lanes):
        own = slice(block * lanes, (block + 1) * lanes)
        diag[own, :] = jnp.broadcast_to(diag_ref[0, :, own], (lanes, lanes)).T
    load_rhs.wait()
    load_factor.wait()
    for copy in load_w:
        copy.wait()

    for outer in range(ITERS):
        for part in (upper, lower):
            res[part, :] = residual(part)
        u[lower, :] = u[lower, :] + OMEGA * res[lower, :]
        ub[lower, :] = u[lower, :].astype(jnp.bfloat16)
        ready[...] = jnp.dot(w[lower, lower], ub[lower, :], preferred_element_type=jnp.float32)
        for k in SEND_ORDER:
            own = slice(k * nodes, (k + 1) * nodes)
            lat_copy(outer, k).wait_recv()
            new = u[own, :] + OMEGA * (res[own, :] + COUPLE * lat_in[outer, k])
            u[own, :] = new
            ub[own, :] = new.astype(jnp.bfloat16)
            if k != SEND_ORDER[-1]:
                ready[...] = ready[...] + jnp.dot(
                    w[lower, own], ub[own, :], preferred_element_type=jnp.float32
                )
        for turn in range(RADIAL_PASSES):
            sweep = outer * RADIAL_PASSES + turn
            bottom = slice(4 * nodes, 5 * nodes)
            top = slice(5 * nodes, 6 * nodes)
            last = slice(SEND_ORDER[-1] * nodes, (SEND_ORDER[-1] + 1) * nodes) if turn == 0 else lower
            applied = ready[...] + jnp.dot(
                w[lower, last], ub[last, :], preferred_element_type=jnp.float32
            )
            res[lower, :] = rhs[lower, :] - (applied + diag[lower, :] * u[lower, :])

            @pl.when(r > 0)
            def _():
                dn_out[sweep] = res[bottom, :]
                dn_copy(sweep).start()

            @pl.when(r == 0)
            def _():
                h_out[sweep] = factor[...] * res[top, :]
                for c in range(CHUNKS):
                    h_copy(sweep, c).start()

            new = u[upper, :] + OMEGA * residual(upper)
            u[upper, :] = new
            ub[upper, :] = new.astype(jnp.bfloat16)
            if turn == RADIAL_PASSES - 1:
                if outer < ITERS - 1:
                    for k in SEND_ORDER:
                        make_faces(outer + 1, (k,))
                        start_faces(outer + 1, (k,))
            else:
                ready[...] = jnp.dot(w[lower, upper], ub[upper, :], preferred_element_type=jnp.float32)

            @pl.when(r > 0)
            def _():
                for c in range(CHUNKS):
                    rows = slice(c * size, (c + 1) * size)
                    from_bottom = slice(4 * nodes + c * size, 4 * nodes + (c + 1) * size)
                    from_top = slice(5 * nodes + c * size, 5 * nodes + (c + 1) * size)
                    h_copy(sweep, c).wait_recv()

                    @pl.when(r < rad_count - 1)
                    def _():
                        h_out[sweep, rows] = factor[rows, :] * (h_in[sweep, rows] + res[from_top, :])
                        h_copy(sweep, c).start()

                    u[from_bottom, :] = u[from_bottom, :] + OMEGA * (
                        res[from_bottom, :] + COUPLE * h_in[sweep, rows]
                    )

            @pl.when(r == 0)
            def _():
                u[bottom, :] = u[bottom, :] + OMEGA * res[bottom, :]

            @pl.when(r < rad_count - 1)
            def _():
                dn_copy(sweep).wait_recv()
                u[top, :] = u[top, :] + OMEGA * (res[top, :] + COUPLE * dn_in[sweep])

            @pl.when(r == rad_count - 1)
            def _():
                u[top, :] = u[top, :] + OMEGA * res[top, :]

            ub[lower, :] = u[lower, :].astype(jnp.bfloat16)

    for outer in range(ITERS):
        for k in SEND_ORDER:
            lat_copy(outer, k).wait_send()

    @pl.when(r > 0)
    def _():
        for sweep in range(ITERS * RADIAL_PASSES):
            dn_copy(sweep).wait_send()

    @pl.when(r < rad_count - 1)
    def _():
        for sweep in range(ITERS * RADIAL_PASSES):
            for c in range(CHUNKS):
                h_copy(sweep, c).wait_send()


def per_device(lat_count, rad_count, schur_off, schur_diag, source, start, decay, neighbour_face, orientation):
    order, columns = source.shape[2:]
    nodes = order // 6
    sweeps = ITERS * RADIAL_PASSES
    faces = lambda *lead: pltpu.VMEM((*lead, nodes, columns), jnp.float32)
    dma = lambda *shape: pltpu.SemaphoreType.DMA(shape)
    smem = pl.BlockSpec(memory_space=pltpu.SMEM)
    vmem = pl.BlockSpec(memory_space=pltpu.VMEM)
    hbm = pl.BlockSpec(memory_space=pl.ANY)
    return pl.pallas_call(
        functools.partial(kernel, lat_count, rad_count, nodes),
        out_shape=jax.ShapeDtypeStruct(source.shape, jnp.float32),
        in_specs=[smem, smem, vmem, hbm, hbm, hbm, hbm],
        out_specs=vmem,
        scratch_shapes=[
            pltpu.VMEM((order, order), jnp.bfloat16),
            pltpu.VMEM((order, columns), jnp.bfloat16),
            pltpu.VMEM((order, columns), jnp.float32),
            faces(),
            pltpu.VMEM((order, columns), jnp.float32),
            pltpu.VMEM((order, columns), jnp.float32),
            pltpu.VMEM((2 * nodes, columns), jnp.float32),
            faces(ITERS, 4), faces(ITERS, 4), faces(sweeps), faces(sweeps), faces(sweeps), faces(sweeps),
            dma(3), dma(2),
            dma(ITERS, 4), dma(ITERS, 4), dma(sweeps), dma(sweeps),
            dma(sweeps, CHUNKS), dma(sweeps, CHUNKS),
        ],
        compiler_params=pltpu.CompilerParams(
            collective_id=0, has_side_effects=True, vmem_limit_bytes=63 * 1024 * 1024
        ),
        name="shell",
    )(neighbour_face.T, orientation.T, schur_diag, schur_off, source, start, decay)


def solution(mesh):
    lat_count, rad_count = mesh.shape["lat"], mesh.shape["rad"]
    return jax.shard_map(
        functools.partial(per_device, lat_count, rad_count),
        mesh=mesh,
        in_specs=(
            P("lat", "rad", None, None),
            P("lat", "rad", None),
            P("lat", "rad", None, None),
            P("lat", "rad", None, None),
            P("lat", "rad", None, None),
            P(),
            P(),
        ),
        out_specs=P("lat", "rad", None, None),
        check_vma=False,
    )
```

profile of v0, /device:TPU:24, one launch (start us, length us, event | category | flops | bytes accessed | tf_op | source)
XLA Modules:
  0.0 50.0 jit_solution(14798487892841765213)
XLA Ops:
  0.0 47.9 %shell.1 = f32[1,1,1536,128]{3,2,1,0:T(8,128)} custom-call(s32[4,8]{1,0:T(4,128)} %bitcast.2, s32[4,8]{1,0:T(4,128)} %bitcast.3, f32[1,1,1536]{2,1,0:T(1,128)} %diag_ref.1, bf16[1,1,1536,1536]{3,2,1,0:T(8,128)(2,1)} %w_hbm.1, f32[1,1,1536,128]{3,2,1,0:T(8,128)} %source_hbm.1, f32[1,1,1536,128]{3,2,1,0:T(8,128)} %start_hbm.1, f32[1,1,256,128]{3,2,1,0:T(8,128)} %decay_hbm.1), custom_call_target="tpu_custom_call" | custom-call | tf_op jit(solution)/shard_map/shell/pallas_call | solution.py:252
  47.9 2.1 %copy.9 = f32[1,1,1536,128]{3,2,1,0:T(8,128)} copy(f32[1,1,1536,128]{3,2,1,0:T(8,128)} %shell.1) | data formatting | bytes 1572864
where the time goes:
time: 50.2 us; the launch traced here: 50 us
  Pallas kernels  47.9 us (95%)
  local copies, waits for them, and re-layouts  2.06 us (4%)
    pallas_call x1, Pallas kernels, per_device(): pl.pallas_call(functools.partial(kernel, lat_count, rad_count, nodes), ou...  47.9 us
    unnamed x1, local copies, waits for them, and re-layouts  2.06 us

commit v1 on v0

--- a/solution.py
+++ b/solution.py
@@ -268,10 +268,13 @@
             dma(sweeps, CHUNKS), dma(sweeps, CHUNKS),
         ],
         compiler_params=pltpu.CompilerParams(
-            collective_id=0, has_side_effects=True, vmem_limit_bytes=63 * 1024 * 1024
+            collective_id=0, has_side_effects=True, vmem_limit_bytes=24 * 1024 * 1024
         ),
         name="shell",
-    )(neighbour_face.T, orientation.T, schur_diag, schur_off, source, start, decay)
+    )(*(
+        pltpu.with_memory_space_constraint(x, pltpu.HBM)
+        for x in (neighbour_face.T, orientation.T, schur_diag, schur_off, source, start, decay)
+    ))
 
 
 def solution(mesh):

time: 50.2 us -> 48.1 us (0.958)
  local copies, waits for them, and re-layouts: 2.06 us -> 0.88 us
  Pallas kernels: 47.9 us -> 47 us
    unnamed x1, local copies, waits for them, and re-layouts: 2.06 us -> 0.88 us
    pallas_call x1, Pallas kernels: 47.9 us -> 47 us  [per_device(): pl.pallas_call(functools.partial(kernel, lat_count, rad_count, nodes), ou...]
where the time goes in v1:
time: 48.1 us; the launch traced here: 47.9 us
  Pallas kernels  47 us (98%)
  local copies, waits for them, and re-layouts  0.88 us (2%)
    pallas_call x1, Pallas kernels, per_device(): pl.pallas_call(functools.partial(kernel, lat_count, rad_count, nodes), ou...  47 us

profile of v1, /device:TPU:24, one launch (start us, length us, event | category | flops | bytes accessed | tf_op | source)
XLA Modules:
  0.0 47.9 jit_solution(1442144700073710357)
XLA Ops:
  0.0 47.0 %shell.1 = f32[1,1,1536,128]{3,2,1,0:T(8,128)S(1)} custom-call(s32[4,8]{1,0:T(4,128)} %bitcast.2, s32[4,8]{1,0:T(4,128)} %bitcast.3, f32[1,1,1536]{2,1,0:T(1,128)} %diag_ref.1, bf16[1,1,1536,1536]{3,2,1,0:T(8,128)(2,1)} %w_hbm.1, f32[1,1,1536,128]{3,2,1,0:T(8,128)} %source_hbm.1, f32[1,1,1536,128]{3,2,1,0:T(8,128)} %start_hbm.1, f32[1,1,256,128]{3,2,1,0:T(8,128)} %decay_hbm.1), custom_call_target="tpu_custom_call" | custom-call | tf_op jit(solution)/shard_map/shell/pallas_call | solution.py:252
  47.0 0.9 %copy.9 = f32[1,1,1536,128]{3,2,1,0:T(8,128)} copy(f32[1,1,1536,128]{3,2,1,0:T(8,128)S(1)} %shell.1) | data formatting | bytes 1572864

commit v2 on v1

v2 whole, which is shorter than its diff:
```python
import contextlib
import functools
import math

import jax
import jax.numpy as jnp
from jax import lax
from jax.experimental import pallas as pl
from jax.experimental.pallas import tpu as pltpu
from jax.sharding import PartitionSpec as P

ITERS = 2
RADIAL_PASSES = 2
OMEGA = 0.3
COUPLE = 0.5
CHUNKS = 8
SEND_ORDER = (2, 3, 0, 1)
MESH = pl.DeviceIdType.MESH


def scope(name):
    return contextlib.nullcontext()


def one_hot(code, side):
    nodes = side * side
    n = lax.broadcasted_iota(jnp.int32, (nodes, 1), 0)
    i, j = n // side, n % side
    swap, rows, cols = code & 1, (code >> 1) & 1, (code >> 2) & 1
    a = i + swap * (j - i)
    b = j + swap * (i - j)
    a = a + rows * (side - 1 - 2 * a)
    b = b + cols * (side - 1 - 2 * b)
    at = lax.broadcasted_iota(jnp.int32, (nodes, nodes), 1)
    return jnp.where(at == a * side + b, 1.0, 0.0).astype(jnp.bfloat16)


def permuted(hot, face):
    high = face.astype(jnp.bfloat16)
    rest = face - high.astype(jnp.float32)
    middle = rest.astype(jnp.bfloat16)
    low = (rest - middle.astype(jnp.float32)).astype(jnp.bfloat16)
    total = None
    for part in (low, middle, high):
        moved = jnp.dot(hot, part, preferred_element_type=jnp.float32)
        total = moved if total is None else total + moved
    return total


def kernel(
    lat_count, rad_count, nodes,
    face_hbm, code_hbm, diag_hbm, w_hbm, source_hbm, start_hbm, decay_hbm,
    out_hbm,
    face_at, code_at, diag_row, w, u, ub, rhs, factor, diag, acc, res_top, hot,
    lat_out, lat_in, dn_out, dn_in, h_out, h_in,
    small_sem, load_sem, w_sem, out_sem,
    lat_send, lat_recv, dn_send, dn_recv, h_send, h_recv,
):
    side = math.isqrt(nodes)
    far = max(2, lat_count // 8)
    offsets = (-1, 1, -far, far)
    p = lax.axis_index("lat")
    r = lax.axis_index("rad")
    size = nodes // CHUNKS
    lanes = u.shape[1]
    upper, lower, every = slice(0, 4 * nodes), slice(4 * nodes, 6 * nodes), slice(0, 6 * nodes)
    bottom, top = slice(4 * nodes, 5 * nodes), slice(5 * nodes, 6 * nodes)

    load_face = pltpu.make_async_copy(face_hbm, face_at, small_sem.at[0])
    load_code = pltpu.make_async_copy(code_hbm, code_at, small_sem.at[1])
    load_diag = pltpu.make_async_copy(diag_hbm.at[0], diag_row, small_sem.at[2])
    load_u = pltpu.make_async_copy(start_hbm.at[0, 0], u, load_sem.at[0])
    load_rhs = pltpu.make_async_copy(source_hbm.at[0, 0], rhs, load_sem.at[1])
    load_factor = pltpu.make_async_copy(decay_hbm.at[0, 0], factor, load_sem.at[2])
    load_w = [
        pltpu.make_async_copy(w_hbm.at[0, 0, part], w.at[part], w_sem.at[n])
        for n, part in enumerate((upper, lower))
    ]
    load_face.start()
    load_code.start()
    load_u.start()

    barrier = pltpu.get_barrier_semaphore()
    for offset in offsets:
        target = (p - offset + lat_count) % lat_count
        pl.semaphore_signal(barrier, inc=1, device_id={"lat": target}, device_id_type=MESH)

    below, above = (r - 1 + rad_count) % rad_count, (r + 1) % rad_count
    first_layer, last_layer = r == 0, r == rad_count - 1
    inner_layer = jnp.logical_and(r > 0, r < rad_count - 1)

    @pl.when(r > 0)
    def _():
        pl.semaphore_signal(barrier, inc=1, device_id={"rad": below}, device_id_type=MESH)

    @pl.when(r < rad_count - 1)
    def _():
        pl.semaphore_signal(barrier, inc=1, device_id={"rad": above}, device_id_type=MESH)

    load_diag.start()
    for copy in load_w:
        copy.start()
    load_rhs.start()
    load_factor.start()

    inner = (r + rad_count - 1) // rad_count + (2 * rad_count - 2 - r) // rad_count

    def lat_copy(outer, k):
        target = (p - offsets[k] + lat_count) % lat_count
        return pltpu.make_async_remote_copy(
            src_ref=lat_out.at[outer, k], dst_ref=lat_in.at[outer, k],
            send_sem=lat_send.at[outer, k], recv_sem=lat_recv.at[outer, k],
            device_id={"lat": target}, device_id_type=MESH,
        )

    def lat_arrival(outer, k):
        return pltpu.make_async_remote_copy(
            src_ref=lat_out.at[outer, k], dst_ref=lat_in.at[outer, k],
            send_sem=lat_send.at[outer, k], recv_sem=lat_recv.at[outer, k],
            device_id={"lat": (p + 1) % lat_count}, device_id_type=MESH,
        )

    def dn_copy(sweep):
        return pltpu.make_async_remote_copy(
            src_ref=dn_out.at[sweep], dst_ref=dn_in.at[sweep],
            send_sem=dn_send.at[sweep], recv_sem=dn_recv.at[sweep],
            device_id={"rad": below}, device_id_type=MESH,
        )

    def h_copy(sweep, c):
        rows = pl.ds(c * size, size)
        return pltpu.make_async_remote_copy(
            src_ref=h_out.at[sweep, rows], dst_ref=h_in.at[sweep, rows],
            send_sem=h_send.at[sweep, c], recv_sem=h_recv.at[sweep, c],
            device_id={"rad": above}, device_id_type=MESH,
        )

    def make_hot(k):
        target = (p - offsets[k] + lat_count) % lat_count
        hot[k] = one_hot(code_at[k, target], side)

    def make_face(outer, k):
        target = (p - offsets[k] + lat_count) % lat_count
        which = jnp.full((nodes, lanes), face_at[k, target], jnp.int32)
        face = u[slice(0, nodes), :]
        for f in range(1, 4):
            face = jnp.where(which == f, u[slice(f * nodes, (f + 1) * nodes), :], face)
        lat_out[outer, k] = permuted(hot[k], face)

    def product(rows, columns):
        return jnp.dot(w[rows, columns], ub[columns, :], preferred_element_type=jnp.float32)

    def residual(rows):
        return rhs[rows, :] - (acc[rows, :] + diag[rows, :] * u[rows, :])

    def round_u(rows):
        ub[rows, :] = u[rows, :].astype(jnp.bfloat16)

    def send_low(sweep):
        res = residual(bottom)
        dn_out[sweep] = res
        u[bottom, :] = u[bottom, :] + OMEGA * res

        @pl.when(r > 0)
        def _():
            dn_copy(sweep).start()

        res = residual(top)
        res_top[...] = res
        u[top, :] = u[top, :] + OMEGA * res

        @pl.when(first_layer)
        def _():
            h_out[sweep] = factor[...] * res_top[...]
            for c in range(CHUNKS):
                h_copy(sweep, c).start()

    def update_upper():
        u[upper, :] = u[upper, :] + OMEGA * residual(upper)
        round_u(upper)

    def take_h(sweep, relay):
        for c in range(CHUNKS):
            rows = slice(c * size, (c + 1) * size)
            from_bottom = slice(4 * nodes + c * size, 4 * nodes + (c + 1) * size)
            with scope("wh%d" % c):
                h_copy(sweep, c).wait_recv()
            if relay:
                h_out[sweep, rows] = factor[rows, :] * (h_in[sweep, rows] + res_top[rows, :])
                h_copy(sweep, c).start()
            u[from_bottom, :] = u[from_bottom, :] + OMEGA * COUPLE * h_in[sweep, rows]

    def take_dn(sweep):
        with scope("wdn"):
            dn_copy(sweep).wait_recv()
        u[top, :] = u[top, :] + OMEGA * COUPLE * dn_in[sweep]

    def add(rows, columns):
        acc[rows, :] = acc[rows, :] + product(rows, columns)

    def exchange_low(sweep, urgent, then, rest):
        @pl.when(first_layer)
        def _():
            round_u(bottom)
            add(every, bottom)
            take_dn(sweep)
            round_u(top)
            with scope("finish"):
                add(urgent, top)

        @pl.when(last_layer)
        def _():
            round_u(top)
            add(every, top)
            take_h(sweep, False)
            round_u(bottom)
            with scope("finish"):
                add(urgent, bottom)

        @pl.when(inner_layer)
        def _():
            take_h(sweep, True)
            take_dn(sweep)
            round_u(lower)
            with scope("finish"):
                add(urgent, lower)

        then()

        @pl.when(first_layer)
        def _():
            add(rest, top)

        @pl.when(last_layer)
        def _():
            add(rest, bottom)

        @pl.when(inner_layer)
        def _():
            add(rest, lower)

    load_face.wait()
    load_code.wait()
    for k in SEND_ORDER:
        make_hot(k)
    with scope("loadu"):
        load_u.wait()
    with scope("mkf"):
        make_face(0, SEND_ORDER[0])
    with scope("bar"):
        pl.semaphore_wait(barrier, len(offsets) + inner)
    lat_copy(0, SEND_ORDER[0]).start()
    with scope("mkf2"):
        for k in SEND_ORDER[1:]:
            make_face(0, k)
            lat_copy(0, k).start()
    round_u(every)
    load_diag.wait()
    for block in range(6 * nodes // lanes):
        own = slice(block * lanes, (block + 1) * lanes)
        diag[own, :] = jnp.broadcast_to(diag_row[:, own], (lanes, lanes)).T
    with scope("waitw"):
        load_rhs.wait()
        load_factor.wait()
        for copy in load_w:
            copy.wait()
    with scope("acc0"):
        acc[...] = product(every, every)

    near = lax.rem(p, 2)
    for outer in range(ITERS):
        with scope("lres"):
            u[...] = u[...] + OMEGA * residual(every)
            round_u(lower)
        with scope("lacc"):
            acc[...] = product(every, lower)
        arrivals = (1 - near, 2, 3, near)
        for turn, k in enumerate(arrivals):
            own = pl.ds(pl.multiple_of(k * nodes, nodes), nodes)
            with scope("wlat%d" % turn):
                lat_arrival(outer, k).wait_recv()
            with scope("alat%d" % turn):
                u[own, :] = u[own, :] + OMEGA * COUPLE * lat_in[outer, k]
                round_u(own)
                add(every if turn < 3 else lower, own)
        sweep = outer * RADIAL_PASSES
        with scope("sendlow"):
            send_low(sweep)
        with scope("resup"):
            add(upper, pl.ds(pl.multiple_of(near * nodes, nodes), nodes))
            update_upper()
        with scope("accup"):
            acc[...] = product(every, upper)

        if outer < ITERS - 1:

            def then():
                with scope("resup2"):
                    update_upper()
                with scope("mkf3"):
                    for k in SEND_ORDER:
                        make_face(outer + 1, k)
                        lat_copy(outer + 1, k).start()

            exchange_low(sweep, upper, then, lower)
            with scope("sendlow2"):
                send_low(sweep + 1)
            with scope("accup2"):
                acc[...] = product(every, upper)

            @pl.when(first_layer)
            def _():
                round_u(bottom)
                add(every, bottom)
                take_dn(sweep + 1)
                round_u(top)
                add(every, top)

            @pl.when(last_layer)
            def _():
                round_u(top)
                add(every, top)
                take_h(sweep + 1, False)
                round_u(bottom)
                add(every, bottom)

            @pl.when(inner_layer)
            def _():
                take_h(sweep + 1, True)
                take_dn(sweep + 1)
                round_u(lower)
                add(every, lower)
        else:

            def then():
                with scope("sendlow3"):
                    send_low(sweep + 1)

            exchange_low(sweep, lower, then, upper)
            with scope("lastup"):
                u[upper, :] = u[upper, :] + OMEGA * residual(upper)
    final = ITERS * RADIAL_PASSES - 1
    stores = [
        pltpu.make_async_copy(u.at[part], out_hbm.at[0, 0, part], out_sem.at[n])
        for n, part in enumerate((upper, bottom, top))
    ]
    stores[0].start()

    @pl.when(first_layer)
    def _():
        stores[1].start()
        take_dn(final)
        stores[2].start()

    @pl.when(last_layer)
    def _():
        stores[2].start()
        take_h(final, False)
        stores[1].start()

    @pl.when(inner_layer)
    def _():
        take_h(final, True)
        stores[1].start()
        take_dn(final)
        stores[2].start()

    with scope("wsend"):
        for outer in range(ITERS):
            for k in SEND_ORDER:
                lat_copy(outer, k).wait_send()

        @pl.when(r > 0)
        def _():
            for sweep in range(ITERS * RADIAL_PASSES):
                dn_copy(sweep).wait_send()

        @pl.when(r < rad_count - 1)
        def _():
            for sweep in range(ITERS * RADIAL_PASSES):
                for c in range(CHUNKS):
                    h_copy(sweep, c).wait_send()

    with scope("wout"):
        for copy in stores:
            copy.wait()


def per_device(lat_count, rad_count, schur_off, schur_diag, source, start, decay, neighbour_face, orientation):
    order, columns = source.shape[2:]
    nodes = order // 6
    sweeps = ITERS * RADIAL_PASSES
    patches, contacts = neighbour_face.shape
    faces = lambda *lead: pltpu.VMEM((*lead, nodes, columns), jnp.float32)
    wide = lambda dtype: pltpu.VMEM((order, columns), dtype)
    dma = lambda *shape: pltpu.SemaphoreType.DMA(shape)
    hbm = pl.BlockSpec(memory_space=pltpu.HBM)
    return pl.pallas_call(
        functools.partial(kernel, lat_count, rad_count, nodes),
        out_shape=jax.ShapeDtypeStruct(source.shape, jnp.float32),
        in_specs=[hbm] * 7,
        out_specs=pl.BlockSpec(memory_space=pl.ANY),
        scratch_shapes=[
            pltpu.SMEM((contacts, patches), jnp.int32),
            pltpu.SMEM((contacts, patches), jnp.int32),
            pltpu.VMEM((1, order), jnp.float32),
            pltpu.VMEM((order, order), jnp.bfloat16),
            wide(jnp.float32),
            wide(jnp.bfloat16),
            wide(jnp.float32),
            faces(),
            wide(jnp.float32),
            wide(jnp.float32),
            faces(),
            pltpu.VMEM((4, nodes, nodes), jnp.bfloat16),
            faces(ITERS, 4), faces(ITERS, 4), faces(sweeps), faces(sweeps), faces(sweeps), faces(sweeps),
            dma(3), dma(3), dma(2), dma(3),
            dma(ITERS, 4), dma(ITERS, 4), dma(sweeps), dma(sweeps),
            dma(sweeps, CHUNKS), dma(sweeps, CHUNKS),
        ],
        compiler_params=pltpu.CompilerParams(
            collective_id=0, has_side_effects=True, vmem_limit_bytes=24 * 1024 * 1024
        ),
        name="shell",
    )(*(
        pltpu.with_memory_space_constraint(x, pltpu.HBM)
        for x in (neighbour_face.T, orientation.T, schur_diag, schur_off, source, start, decay)
    ))


def solution(mesh):
    lat_count, rad_count = mesh.shape["lat"], mesh.shape["rad"]
    return jax.shard_map(
        functools.partial(per_device, lat_count, rad_count),
        mesh=mesh,
        in_specs=(
            P("lat", "rad", None, None),
            P("lat", "rad", None),
            P("lat", "rad", None, None),
            P("lat", "rad", None, None),
            P("lat", "rad", None, None),
            P(),
            P(),
        ),
        out_specs=P("lat", "rad", None, None),
        check_vma=False,
    )
```

time: 48.1 us -> 44.8 us (0.931)
  Pallas kernels: 47 us -> 43.3 us
    pallas_call x1, Pallas kernels: 47 us -> 43.3 us  [per_device(): pl.pallas_call(functools.partial(kernel, lat_count, rad_count, nodes), ou...]
where the time goes in v2:
time: 44.8 us; the launch traced here: 44.2 us
  Pallas kernels  43.3 us (97%)
  local copies, waits for them, and re-layouts  0.88 us (2%)
    pallas_call x1, Pallas kernels, per_device(): pl.pallas_call(functools.partial(kernel, lat_count, rad_count, nodes), ou...  43.3 us

profile of v2, /device:TPU:24, one launch (start us, length us, event | category | flops | bytes accessed | tf_op | source)
XLA Modules:
  0.0 44.2 jit_solution(2149023582895867149)
XLA Ops:
  0.0 43.3 %shell.1 = f32[1,1,1536,128]{3,2,1,0:T(8,128)S(1)} custom-call(s32[4,8]{1,0:T(4,128)} %bitcast.2, s32[4,8]{1,0:T(4,128)} %bitcast.3, f32[1,1,1536]{2,1,0:T(1,128)} %diag_hbm.1, bf16[1,1,1536,1536]{3,2,1,0:T(8,128)(2,1)} %w_hbm.1, f32[1,1,1536,128]{3,2,1,0:T(8,128)} %source_hbm.1, f32[1,1,1536,128]{3,2,1,0:T(8,128)} %start_hbm.1, f32[1,1,256,128]{3,2,1,0:T(8,128)} %decay_hbm.1), custom_call_target="tpu_custom_call" | custom-call | tf_op jit(solution)/shard_map/shell/pallas_call | solution.py:398
  43.3 0.9 %copy.9 = f32[1,1,1536,128]{3,2,1,0:T(8,128)} copy(f32[1,1,1536,128]{3,2,1,0:T(8,128)S(1)} %shell.1) | data formatting | bytes 1572864

commit v3 on v2

--- a/solution.py
+++ b/solution.py
@@ -13,7 +13,7 @@
 RADIAL_PASSES = 2
 OMEGA = 0.3
 COUPLE = 0.5
-CHUNKS = 8
+CHUNKS = 16
 SEND_ORDER = (2, 3, 0, 1)
 MESH = pl.DeviceIdType.MESH
 
@@ -109,21 +109,21 @@
         target = (p - offsets[k] + lat_count) % lat_count
         return pltpu.make_async_remote_copy(
             src_ref=lat_out.at[outer, k], dst_ref=lat_in.at[outer, k],
-            send_sem=lat_send.at[outer, k], recv_sem=lat_recv.at[outer, k],
+            send_sem=lat_send.at[outer], recv_sem=lat_recv.at[outer, k],
             device_id={"lat": target}, device_id_type=MESH,
         )
 
     def lat_arrival(outer, k):
         return pltpu.make_async_remote_copy(
             src_ref=lat_out.at[outer, k], dst_ref=lat_in.at[outer, k],
-            send_sem=lat_send.at[outer, k], recv_sem=lat_recv.at[outer, k],
+            send_sem=lat_send.at[outer], recv_sem=lat_recv.at[outer, k],
             device_id={"lat": (p + 1) % lat_count}, device_id_type=MESH,
         )
 
     def dn_copy(sweep):
         return pltpu.make_async_remote_copy(
             src_ref=dn_out.at[sweep], dst_ref=dn_in.at[sweep],
-            send_sem=dn_send.at[sweep], recv_sem=dn_recv.at[sweep],
+            send_sem=dn_send.at[sweep], recv_sem=dn_recv.at[sweep % 2],
             device_id={"rad": below}, device_id_type=MESH,
         )
 
@@ -131,7 +131,21 @@
         rows = pl.ds(c * size, size)
         return pltpu.make_async_remote_copy(
             src_ref=h_out.at[sweep, rows], dst_ref=h_in.at[sweep, rows],
-            send_sem=h_send.at[sweep, c], recv_sem=h_recv.at[sweep, c],
+            send_sem=h_send.at[sweep], recv_sem=h_recv.at[sweep % 2, c],
+            device_id={"rad": above}, device_id_type=MESH,
+        )
+
+    def lat_sent(outer):
+        return pltpu.make_async_remote_copy(
+            src_ref=lat_out.at[outer], dst_ref=lat_in.at[outer],
+            send_sem=lat_send.at[outer], recv_sem=lat_recv.at[outer, 0],
+            device_id={"lat": (p + 1) % lat_count}, device_id_type=MESH,
+        )
+
+    def h_sent(sweep):
+        return pltpu.make_async_remote_copy(
+            src_ref=h_out.at[sweep], dst_ref=h_in.at[sweep],
+            send_sem=h_send.at[sweep], recv_sem=h_recv.at[sweep % 2, 0],
             device_id={"rad": above}, device_id_type=MESH,
         )
 
@@ -195,8 +209,16 @@
             dn_copy(sweep).wait_recv()
         u[top, :] = u[top, :] + OMEGA * COUPLE * dn_in[sweep]
 
+    def blocks(rows):
+        return [slice(at, at + nodes) for at in range(rows.start, rows.stop, nodes)]
+
     def add(rows, columns):
-        acc[rows, :] = acc[rows, :] + product(rows, columns)
+        for block in blocks(rows):
+            acc[block, :] = acc[block, :] + product(block, columns)
+
+    def begin(columns):
+        for block in blocks(every):
+            acc[block, :] = product(block, columns)
 
     def exchange_low(sweep, urgent, then, rest):
         @pl.when(first_layer)
@@ -265,7 +287,7 @@
         for copy in load_w:
             copy.wait()
     with scope("acc0"):
-        acc[...] = product(every, every)
+        begin(every)
 
     near = lax.rem(p, 2)
     for outer in range(ITERS):
@@ -273,7 +295,7 @@
             u[...] = u[...] + OMEGA * residual(every)
             round_u(lower)
         with scope("lacc"):
-            acc[...] = product(every, lower)
+            begin(lower)
         arrivals = (1 - near, 2, 3, near)
         for turn, k in enumerate(arrivals):
             own = pl.ds(pl.multiple_of(k * nodes, nodes), nodes)
@@ -290,7 +312,7 @@
             add(upper, pl.ds(pl.multiple_of(near * nodes, nodes), nodes))
             update_upper()
         with scope("accup"):
-            acc[...] = product(every, upper)
+            begin(upper)
 
         if outer < ITERS - 1:
 
@@ -306,7 +328,7 @@
             with scope("sendlow2"):
                 send_low(sweep + 1)
             with scope("accup2"):
-                acc[...] = product(every, upper)
+                begin(upper)
 
             @pl.when(first_layer)
             def _():
@@ -367,8 +389,7 @@
 
     with scope("wsend"):
         for outer in range(ITERS):
-            for k in SEND_ORDER:
-                lat_copy(outer, k).wait_send()
+            lat_sent(outer).wait_send()
 
         @pl.when(r > 0)
         def _():
@@ -378,8 +399,7 @@
         @pl.when(r < rad_count - 1)
         def _():
             for sweep in range(ITERS * RADIAL_PASSES):
-                for c in range(CHUNKS):
-                    h_copy(sweep, c).wait_send()
+                h_sent(sweep).wait_send()
 
     with scope("wout"):
         for copy in stores:
@@ -415,8 +435,8 @@
             pltpu.VMEM((4, nodes, nodes), jnp.bfloat16),
             faces(ITERS, 4), faces(ITERS, 4), faces(sweeps), faces(sweeps), faces(sweeps), faces(sweeps),
             dma(3), dma(3), dma(2), dma(3),
-            dma(ITERS, 4), dma(ITERS, 4), dma(sweeps), dma(sweeps),
-            dma(sweeps, CHUNKS), dma(sweeps, CHUNKS),
+            dma(ITERS), dma(ITERS, 4), dma(sweeps), dma(2),
+            dma(sweeps), dma(2, CHUNKS),
         ],
         compiler_params=pltpu.CompilerParams(
             collective_id=0, has_side_effects=True, vmem_limit_bytes=24 * 1024 * 1024

time: 44.8 us -> 44 us (0.982)
  Pallas kernels: 43.3 us -> 42.5 us
    pallas_call x1, Pallas kernels: 43.3 us -> 42.5 us  [per_device(): pl.pallas_call(functools.partial(kernel, lat_count, rad_count, nodes), ou...]
where the time goes in v3:
time: 44 us; the launch traced here: 43.4 us
  Pallas kernels  42.5 us (97%)
  local copies, waits for them, and re-layouts  0.88 us (2%)
    pallas_call x1, Pallas kernels, per_device(): pl.pallas_call(functools.partial(kernel, lat_count, rad_count, nodes), ou...  42.5 us
    unnamed x1, local copies, waits for them, and re-layouts  0.88 us

profile of v3, /device:TPU:24, one launch (start us, length us, event | category | flops | bytes accessed | tf_op | source)
XLA Modules:
  0.0 43.4 jit_solution(787451083873264127)
XLA Ops:
  0.0 42.5 %shell.1 = f32[1,1,1536,128]{3,2,1,0:T(8,128)S(1)} custom-call(s32[4,8]{1,0:T(4,128)} %bitcast.2, s32[4,8]{1,0:T(4,128)} %bitcast.3, f32[1,1,1536]{2,1,0:T(1,128)} %diag_hbm.1, bf16[1,1,1536,1536]{3,2,1,0:T(8,128)(2,1)} %w_hbm.1, f32[1,1,1536,128]{3,2,1,0:T(8,128)} %source_hbm.1, f32[1,1,1536,128]{3,2,1,0:T(8,128)} %start_hbm.1, f32[1,1,256,128]{3,2,1,0:T(8,128)} %decay_hbm.1), custom_call_target="tpu_custom_call" | custom-call | tf_op jit(solution)/shard_map/shell/pallas_call | solution.py:418
  42.5 0.9 %copy.9 = f32[1,1,1536,128]{3,2,1,0:T(8,128)} copy(f32[1,1,1536,128]{3,2,1,0:T(8,128)S(1)} %shell.1) | data formatting | bytes 1572864

commit v4 on v3

v4 whole, which is shorter than its diff:
```python
import contextlib
import functools
import math

import jax
import jax.numpy as jnp
from jax import lax
from jax.experimental import pallas as pl
from jax.experimental.pallas import tpu as pltpu
from jax.sharding import PartitionSpec as P

ITERS = 2
RADIAL_PASSES = 2
OMEGA = 0.3
COUPLE = 0.5
CHUNKS = 8
HALVES = (0, 1)
SEND_ORDER = (2, 3, 0, 1)
MESH = pl.DeviceIdType.MESH


def scope(name):
    return contextlib.nullcontext()


def one_hot(code, side):
    nodes = side * side
    n = lax.broadcasted_iota(jnp.int32, (nodes, 1), 0)
    i, j = n // side, n % side
    swap, rows, cols = code & 1, (code >> 1) & 1, (code >> 2) & 1
    a = i + swap * (j - i)
    b = j + swap * (i - j)
    a = a + rows * (side - 1 - 2 * a)
    b = b + cols * (side - 1 - 2 * b)
    at = lax.broadcasted_iota(jnp.int32, (nodes, nodes), 1)
    return jnp.where(at == a * side + b, 1.0, 0.0).astype(jnp.bfloat16)


def permuted(hot, face):
    high = face.astype(jnp.bfloat16)
    rest = face - high.astype(jnp.float32)
    middle = rest.astype(jnp.bfloat16)
    low = (rest - middle.astype(jnp.float32)).astype(jnp.bfloat16)
    total = None
    for part in (low, middle, high):
        moved = jnp.dot(hot, part, preferred_element_type=jnp.float32)
        total = moved if total is None else total + moved
    return total


def kernel(
    lat_count, rad_count, nodes,
    face_hbm, code_hbm, diag_hbm, w_hbm, source_hbm, start_hbm, decay_hbm,
    out_hbm,
    face_at, code_at, diag_row, w, u, ub, rhs, factor, diag, acc, acc_low, packed_factor, packed_top, hot,
    lat_out, lat_in, dn_out, dn_in, h_out, h_in,
    small_sem, load_sem, w_sem, out_sem,
    lat_send, lat_recv, dn_send, dn_recv, h_send, h_recv,
):
    side = math.isqrt(nodes)
    far = max(2, lat_count // 8)
    offsets = (-1, 1, -far, far)
    p = lax.axis_index("lat")
    r = lax.axis_index("rad")
    lanes = u.shape[1]
    half = lanes // 2
    size = nodes // 2 // CHUNKS
    upper, lower, every = slice(0, 4 * nodes), slice(4 * nodes, 6 * nodes), slice(0, 6 * nodes)
    bottom, top = slice(4 * nodes, 5 * nodes), slice(5 * nodes, 6 * nodes)

    load_face = pltpu.make_async_copy(face_hbm, face_at, small_sem.at[0])
    load_code = pltpu.make_async_copy(code_hbm, code_at, small_sem.at[1])
    load_diag = pltpu.make_async_copy(diag_hbm.at[0], diag_row, small_sem.at[2])
    load_u = pltpu.make_async_copy(start_hbm.at[0, 0], u, load_sem.at[0])
    load_rhs = pltpu.make_async_copy(source_hbm.at[0, 0], rhs, load_sem.at[1])
    load_factor = pltpu.make_async_copy(decay_hbm.at[0, 0], factor, load_sem.at[2])
    load_w = [
        pltpu.make_async_copy(w_hbm.at[0, 0, part], w.at[part], w_sem.at[n])
        for n, part in enumerate((upper, lower))
    ]
    load_face.start()
    load_code.start()
    load_u.start()

    barrier = pltpu.get_barrier_semaphore()
    for offset in offsets:
        target = (p - offset + lat_count) % lat_count
        pl.semaphore_signal(barrier, inc=1, device_id={"lat": target}, device_id_type=MESH)

    below, above = (r - 1 + rad_count) % rad_count, (r + 1) % rad_count
    first_layer, last_layer = r == 0, r == rad_count - 1
    inner_layer = jnp.logical_and(r > 0, r < rad_count - 1)
    second_layer = jnp.logical_and(r == 1, r < rad_count - 1)
    later_layer = jnp.logical_and(r > 1, r < rad_count - 1)

    @pl.when(r > 0)
    def _():
        pl.semaphore_signal(barrier, inc=1, device_id={"rad": below}, device_id_type=MESH)

    @pl.when(r < rad_count - 1)
    def _():
        pl.semaphore_signal(barrier, inc=1, device_id={"rad": above}, device_id_type=MESH)

    load_diag.start()
    for copy in load_w:
        copy.start()
    load_rhs.start()
    load_factor.start()

    inner = (r + rad_count - 1) // rad_count + (2 * rad_count - 2 - r) // rad_count

    def in_half(s, rows):
        lane = lax.broadcasted_iota(jnp.int32, (rows, lanes), 1)
        return lane < half if s == 0 else lane >= half

    def pack(x, s):
        first, second = x[: nodes // 2, :], x[nodes // 2 :, :]
        left = in_half(0, nodes // 2)
        if s == 0:
            return jnp.where(left, first, pltpu.roll(second, half, 1))
        return jnp.where(left, pltpu.roll(first, half, 1), second)

    def unpack(x, s):
        moved = pltpu.roll(x, half, 1)
        return jnp.concatenate([x, moved] if s == 0 else [moved, x], axis=0)

    def gain(rows, value, s):
        u[rows, :] = u[rows, :] + jnp.where(in_half(s, value.shape[0]), value, 0.0)

    def lat_copy(outer, s, k, target):
        return pltpu.make_async_remote_copy(
            src_ref=lat_out.at[outer, s, k], dst_ref=lat_in.at[outer, s, k],
            send_sem=lat_send.at[outer], recv_sem=lat_recv.at[outer, s, k],
            device_id={"lat": target}, device_id_type=MESH,
        )

    def lat_target(k):
        return (p - offsets[k] + lat_count) % lat_count

    def lat_sent(outer):
        return pltpu.make_async_remote_copy(
            src_ref=lat_out.at[outer], dst_ref=lat_in.at[outer],
            send_sem=lat_send.at[outer], recv_sem=lat_recv.at[outer, 0, 0],
            device_id={"lat": (p + 1) % lat_count}, device_id_type=MESH,
        )

    def dn_copy(sweep, s):
        return pltpu.make_async_remote_copy(
            src_ref=dn_out.at[sweep, s], dst_ref=dn_in.at[sweep, s],
            send_sem=dn_send.at[sweep], recv_sem=dn_recv.at[sweep % 2, s],
            device_id={"rad": below}, device_id_type=MESH,
        )

    def dn_sent(sweep):
        return pltpu.make_async_remote_copy(
            src_ref=dn_out.at[sweep], dst_ref=dn_in.at[sweep],
            send_sem=dn_send.at[sweep], recv_sem=dn_recv.at[sweep % 2, 0],
            device_id={"rad": below}, device_id_type=MESH,
        )

    def h_copy(sweep, s, c):
        rows = pl.ds(c * size, size)
        return pltpu.make_async_remote_copy(
            src_ref=h_out.at[sweep, s, rows], dst_ref=h_in.at[sweep, s, rows],
            send_sem=h_send.at[sweep], recv_sem=h_recv.at[sweep % 2, s, c],
            device_id={"rad": above}, device_id_type=MESH,
        )

    def h_sent(sweep):
        return pltpu.make_async_remote_copy(
            src_ref=h_out.at[sweep], dst_ref=h_in.at[sweep],
            send_sem=h_send.at[sweep], recv_sem=h_recv.at[sweep % 2, 0, 0],
            device_id={"rad": above}, device_id_type=MESH,
        )

    def make_hot(k):
        hot[k] = one_hot(code_at[k, lat_target(k)], side)

    def oriented(k):
        which = jnp.full((nodes, lanes), face_at[k, lat_target(k)], jnp.int32)
        face = u[slice(0, nodes), :]
        for f in range(1, 4):
            face = jnp.where(which == f, u[slice(f * nodes, (f + 1) * nodes), :], face)
        return permuted(hot[k], face)

    def send_faces(outer, s):
        for pair in (SEND_ORDER[:2], SEND_ORDER[2:]):
            faces = [pack(oriented(k), s) for k in pair]
            for k, face in zip(pair, faces):
                lat_out[outer, s, k] = face
            for k in pair:
                lat_copy(outer, s, k, lat_target(k)).start()

    def product(rows, columns):
        return jnp.dot(w[rows, columns], ub[columns, :], preferred_element_type=jnp.float32)

    def blocks(rows):
        return [slice(at, at + nodes) for at in range(rows.start, rows.stop, nodes)]

    def add(rows, columns):
        for block in blocks(rows):
            acc[block, :] = acc[block, :] + product(block, columns)

    def begin(columns):
        for block in blocks(every):
            acc[block, :] = product(block, columns)

    def left_over(rows, total):
        return rhs[rows, :] - (total + diag[rows, :] * u[rows, :])

    def residual(rows):
        return left_over(rows, acc[rows, :])

    def round_u(rows):
        ub[rows, :] = u[rows, :].astype(jnp.bfloat16)

    def round_half(rows, s):
        count = rows.stop - rows.start
        old = ub[rows, :].astype(jnp.float32)
        ub[rows, :] = jnp.where(in_half(s, count), u[rows, :], old).astype(jnp.bfloat16)

    def send_low(sweep, s, total):
        res = left_over(bottom, total(bottom))
        dn_out[sweep, s] = pack(res, s)

        @pl.when(r > 0)
        def _():
            dn_copy(sweep, s).start()

        gain(bottom, OMEGA * res, s)
        res = left_over(top, total(top))
        packed_top[s] = pack(res, s)

        @pl.when(first_layer)
        def _():
            h_out[sweep, s] = packed_factor[s] * packed_top[s]
            for c in range(CHUNKS):
                h_copy(sweep, s, c).start()

        gain(top, OMEGA * res, s)

    def relay(where, sweep, s):
        @pl.when(where)
        def _():
            with scope("relay%d%d" % (sweep, s)):
                for c in range(CHUNKS):
                    rows = slice(c * size, (c + 1) * size)
                    h_copy(sweep, s, c).wait_recv()
                    h_out[sweep, s, rows] = packed_factor[s, rows] * (
                        h_in[sweep, s, rows] + packed_top[s, rows]
                    )
                    h_copy(sweep, s, c).start()

    def take(sweep, s):
        @pl.when(last_layer)
        def _():
            with scope("take%d%d" % (sweep, s)):
                for c in range(CHUNKS):
                    h_copy(sweep, s, c).wait_recv()

    def apply_h(sweep, s):
        @pl.when(r > 0)
        def _():
            gain(bottom, OMEGA * COUPLE * unpack(h_in[sweep, s], s), s)

    def apply_dn(sweep, s):
        @pl.when(r < rad_count - 1)
        def _():
            with scope("wdn%d%d" % (sweep, s)):
                dn_copy(sweep, s).wait_recv()
            gain(top, OMEGA * COUPLE * unpack(dn_in[sweep, s], s), s)

    def added(rows):
        return acc[rows, :] + product(rows, lower)

    load_face.wait()
    load_code.wait()
    for k in SEND_ORDER:
        make_hot(k)
    with scope("loadu"):
        load_u.wait()
    with scope("mkf"):
        for k in SEND_ORDER:
            face = oriented(k)
            for s in HALVES:
                lat_out[0, s, k] = pack(face, s)
            if k == SEND_ORDER[0]:
                with scope("bar"):
                    pl.semaphore_wait(barrier, len(offsets) + inner)
            lat_copy(0, 0, k, lat_target(k)).start()
        for k in SEND_ORDER:
            lat_copy(0, 1, k, lat_target(k)).start()
    round_u(every)
    load_diag.wait()
    for block in range(6 * nodes // lanes):
        own = slice(block * lanes, (block + 1) * lanes)
        diag[own, :] = jnp.broadcast_to(diag_row[:, own], (lanes, lanes)).T
    with scope("waitw"):
        load_rhs.wait()
        load_factor.wait()
        for copy in load_w:
            copy.wait()
    for s in HALVES:
        packed_factor[s] = pack(factor[...], s)
    with scope("acc0"):
        begin(every)

    near = lax.rem(p, 2)
    for outer in range(ITERS):
        first, second = outer * RADIAL_PASSES, outer * RADIAL_PASSES + 1
        with scope("lres"):
            u[...] = u[...] + OMEGA * residual(every)
            round_u(lower)
        with scope("lacc"):
            begin(lower)
            acc_low[...] = acc[lower, :]
        for s in HALVES:
            total = acc_low if s == 0 else acc.at[lower]
            for turn, k in enumerate((1 - near, 2, 3, near)):
                own = pl.ds(pl.multiple_of(k * nodes, nodes), nodes)
                with scope("wlat%d%d" % (s, turn)):
                    lat_copy(outer, s, k, (p + 1) % lat_count).wait_recv()
                gain(own, OMEGA * COUPLE * unpack(lat_in[outer, s, k], s), s)
                round_u(own)
                columns = own
                if outer == 1:
                    if turn < 3:
                        continue
                    columns = upper
                for block in (slice(0, nodes), slice(nodes, 2 * nodes)):
                    rows = slice(4 * nodes + block.start, 4 * nodes + block.stop)
                    total[block, :] = total[block, :] + product(rows, columns)
                if outer == 0 and s == 1 and turn == 0:
                    relay(second_layer, first, 0)
            with scope("sendlow%d" % s):
                if s == 0:
                    send_low(first, s, lambda rows: acc_low[rows.start - 4 * nodes : rows.stop - 4 * nodes, :])
                else:
                    send_low(first, s, lambda rows: acc[rows, :])
        if outer == 0:
            relay(later_layer, first, 0)
        with scope("bulk1"):
            add(upper, upper)
            u[upper, :] = u[upper, :] + OMEGA * residual(upper)
            round_u(upper)
        if outer == 1:
            relay(second_layer, first, 0)
        with scope("bulk2"):
            begin(upper)
        relay(second_layer, first, 1)
        if outer == 1:
            relay(later_layer, first, 0)
            relay(later_layer, first, 1)
        for s in HALVES:
            take(first, s)
            apply_h(first, s)
            apply_dn(first, s)
            with scope("fin%d" % s):
                round_half(lower, s)
                if outer < ITERS - 1:
                    for block in blocks(upper):
                        gain(block, OMEGA * left_over(block, added(block)), s)
            with scope("sendlow2%d" % s):
                sums = added(lower)
                send_low(second, s, lambda rows: sums[rows.start - 4 * nodes : rows.stop - 4 * nodes, :])
            if outer < ITERS - 1:
                if s == 0:
                    relay(later_layer, first, 1)
                else:
                    relay(second_layer, second, 0)
                with scope("faces%d" % s):
                    send_faces(outer + 1, s)
        if outer < ITERS - 1:
            relay(later_layer, second, 0)
            relay(inner_layer, second, 1)
            with scope("bulk3"):
                round_u(upper)
                begin(upper)
            for s in HALVES:
                take(second, s)
                apply_h(second, s)
                apply_dn(second, s)
            with scope("bulk4"):
                round_u(lower)
                add(every, lower)
    with scope("lastup"):
        for block in blocks(upper):
            u[block, :] = u[block, :] + OMEGA * left_over(block, added(block))
    final = ITERS * RADIAL_PASSES - 1
    stores = [
        pltpu.make_async_copy(u.at[part], out_hbm.at[0, 0, part], out_sem.at[n])
        for n, part in enumerate((upper, bottom, top))
    ]
    stores[0].start()
    for s in HALVES:
        relay(inner_layer, final, s)
        take(final, s)
        apply_h(final, s)
    stores[1].start()
    for s in HALVES:
        apply_dn(final, s)
    stores[2].start()

    with scope("wsend"):
        for outer in range(ITERS):
            lat_sent(outer).wait_send()

        @pl.when(r > 0)
        def _():
            for sweep in range(ITERS * RADIAL_PASSES):
                dn_sent(sweep).wait_send()

        @pl.when(r < rad_count - 1)
        def _():
            for sweep in range(ITERS * RADIAL_PASSES):
                h_sent(sweep).wait_send()

    with scope("wout"):
        for copy in stores:
            copy.wait()


def per_device(lat_count, rad_count, schur_off, schur_diag, source, start, decay, neighbour_face, orientation):
    order, columns = source.shape[2:]
    nodes = order // 6
    sweeps = ITERS * RADIAL_PASSES
    patches, contacts = neighbour_face.shape
    faces = lambda *lead: pltpu.VMEM((*lead, nodes, columns), jnp.float32)
    packed = lambda *lead: pltpu.VMEM((*lead, 2, nodes // 2, columns), jnp.float32)
    wide = lambda dtype: pltpu.VMEM((order, columns), dtype)
    dma = lambda *shape: pltpu.SemaphoreType.DMA(shape)
    hbm = pl.BlockSpec(memory_space=pltpu.HBM)
    return pl.pallas_call(
        functools.partial(kernel, lat_count, rad_count, nodes),
        out_shape=jax.ShapeDtypeStruct(source.shape, jnp.float32),
        in_specs=[hbm] * 7,
        out_specs=pl.BlockSpec(memory_space=pl.ANY),
        scratch_shapes=[
            pltpu.SMEM((contacts, patches), jnp.int32),
            pltpu.SMEM((contacts, patches), jnp.int32),
            pltpu.VMEM((1, order), jnp.float32),
            pltpu.VMEM((order, order), jnp.bfloat16),
            wide(jnp.float32),
            wide(jnp.bfloat16),
            wide(jnp.float32),
            faces(),
            wide(jnp.float32),
            wide(jnp.float32),
            pltpu.VMEM((2 * nodes, columns), jnp.float32),
            packed(),
            packed(),
            pltpu.VMEM((4, nodes, nodes), jnp.bfloat16),
            pltpu.VMEM((ITERS, 2, 4, nodes // 2, columns), jnp.float32),
            pltpu.VMEM((ITERS, 2, 4, nodes // 2, columns), jnp.float32),
            packed(sweeps), packed(sweeps), packed(sweeps), packed(sweeps),
            dma(3), dma(3), dma(2), dma(3),
            dma(ITERS), dma(ITERS, 2, 4), dma(sweeps), dma(2, 2),
            dma(sweeps), dma(2, 2, CHUNKS),
        ],
        compiler_params=pltpu.CompilerParams(
            collective_id=0, has_side_effects=True, vmem_limit_bytes=24 * 1024 * 1024
        ),
        name="shell",
    )(*(
        pltpu.with_memory_space_constraint(x, pltpu.HBM)
        for x in (neighbour_face.T, orientation.T, schur_diag, schur_off, source, start, decay)
    ))


def solution(mesh):
    lat_count, rad_count = mesh.shape["lat"], mesh.shape["rad"]
    return jax.shard_map(
        functools.partial(per_device, lat_count, rad_count),
        mesh=mesh,
        in_specs=(
            P("lat", "rad", None, None),
            P("lat", "rad", None),
            P("lat", "rad", None, None),
            P("lat", "rad", None, None),
            P("lat", "rad", None, None),
            P(),
            P(),
        ),
        out_specs=P("lat", "rad", None, None),
        check_vma=False,
    )
```

time: 44 us -> 41.3 us (0.939)
  Pallas kernels: 42.5 us -> 39.9 us
    pallas_call x1, Pallas kernels: 42.5 us -> 39.9 us  [per_device(): pl.pallas_call(functools.partial(kernel, lat_count, rad_count, nodes), ou...]
where the time goes in v4:
time: 41.3 us; the launch traced here: 40.8 us
  Pallas kernels  39.9 us (97%)
  local copies, waits for them, and re-layouts  0.88 us (2%)
    pallas_call x1, Pallas kernels, per_device(): pl.pallas_call(functools.partial(kernel, lat_count, rad_count, nodes), ou...  39.9 us
    unnamed x1, local copies, waits for them, and re-layouts  0.88 us

profile of v4, /device:TPU:24, one launch (start us, length us, event | category | flops | bytes accessed | tf_op | source)
XLA Modules:
  0.0 40.8 jit_solution(2372147560853587522)
XLA Ops:
  0.0 39.9 %shell.1 = f32[1,1,1536,128]{3,2,1,0:T(8,128)S(1)} custom-call(s32[4,8]{1,0:T(4,128)} %bitcast.2, s32[4,8]{1,0:T(4,128)} %bitcast.3, f32[1,1,1536]{2,1,0:T(1,128)} %diag_hbm.1, bf16[1,1,1536,1536]{3,2,1,0:T(8,128)(2,1)} %w_hbm.1, f32[1,1,1536,128]{3,2,1,0:T(8,128)} %source_hbm.1, f32[1,1,1536,128]{3,2,1,0:T(8,128)} %start_hbm.1, f32[1,1,256,128]{3,2,1,0:T(8,128)} %decay_hbm.1), custom_call_target="tpu_custom_call" | custom-call | tf_op jit(solution)/shard_map/shell/pallas_call | solution.py:433
  39.9 0.9 %copy.9 = f32[1,1,1536,128]{3,2,1,0:T(8,128)} copy(f32[1,1,1536,128]{3,2,1,0:T(8,128)S(1)} %shell.1) | data formatting | bytes 1572864

commit v5 on v4

--- a/solution.py
+++ b/solution.py
@@ -52,7 +52,7 @@
     lat_count, rad_count, nodes,
     face_hbm, code_hbm, diag_hbm, w_hbm, source_hbm, start_hbm, decay_hbm,
     out_hbm,
-    face_at, code_at, diag_row, w, u, ub, rhs, factor, diag, acc, acc_low, packed_factor, packed_top, hot,
+    face_at, code_at, diag_row, w, u, ub, rhs, factor, diag, sums, packed_factor, packed_top, hot,
     lat_out, lat_in, dn_out, dn_in, h_out, h_in,
     small_sem, load_sem, w_sem, out_sem,
     lat_send, lat_recv, dn_send, dn_recv, h_send, h_recv,
@@ -197,19 +197,16 @@
     def blocks(rows):
         return [slice(at, at + nodes) for at in range(rows.start, rows.stop, nodes)]
 
-    def add(rows, columns):
+    def add(acc, rows, columns):
         for block in blocks(rows):
             acc[block, :] = acc[block, :] + product(block, columns)
 
-    def begin(columns):
-        for block in blocks(every):
+    def begin(acc, rows, columns):
+        for block in blocks(rows):
             acc[block, :] = product(block, columns)
 
     def left_over(rows, total):
         return rhs[rows, :] - (total + diag[rows, :] * u[rows, :])
-
-    def residual(rows):
-        return left_over(rows, acc[rows, :])
 
     def round_u(rows):
         ub[rows, :] = u[rows, :].astype(jnp.bfloat16)
@@ -270,8 +267,34 @@
                 dn_copy(sweep, s).wait_recv()
             gain(top, OMEGA * COUPLE * unpack(dn_in[sweep, s], s), s)
 
-    def added(rows):
-        return acc[rows, :] + product(rows, lower)
+    def arrive(outer, s, k):
+        own = pl.ds(pl.multiple_of(k * nodes, nodes), nodes)
+        with scope("wlat%d" % s):
+            lat_copy(outer, s, k, (p + 1) % lat_count).wait_recv()
+        gain(own, OMEGA * COUPLE * unpack(lat_in[outer, s, k], s), s)
+        round_u(own)
+        return own
+
+    def close(sweep, s, acc):
+        take(sweep, s)
+        apply_h(sweep, s)
+        apply_dn(sweep, s)
+
+    def send_next(sweep, s, acc):
+        with scope("sendnext%d" % s):
+            low = acc[lower, :] + product(lower, lower)
+            send_low(sweep, s, lambda rows: low[rows.start - 4 * nodes : rows.stop - 4 * nodes, :])
+
+    def advance_all(acc):
+        for block in blocks(every):
+            total = acc[block, :] + product(block, lower)
+            u[block, :] = u[block, :] + OMEGA * left_over(block, total)
+
+    def bulk_rows(acc, s):
+        add(acc, upper, upper)
+        for block in blocks(upper):
+            gain(block, OMEGA * left_over(block, acc[block, :]), s)
+        round_u(upper)
 
     load_face.wait()
     load_code.wait()
@@ -302,90 +325,94 @@
             copy.wait()
     for s in HALVES:
         packed_factor[s] = pack(factor[...], s)
+    ahead, behind = sums.at[0], sums.at[1]
     with scope("acc0"):
-        begin(every)
+        for block in blocks(every):
+            u[block, :] = u[block, :] + OMEGA * left_over(block, product(block, every))
 
     near = lax.rem(p, 2)
+    order = (1 - near, 2, 3, near)
     for outer in range(ITERS):
         first, second = outer * RADIAL_PASSES, outer * RADIAL_PASSES + 1
-        with scope("lres"):
-            u[...] = u[...] + OMEGA * residual(every)
-            round_u(lower)
-        with scope("lacc"):
-            begin(lower)
-            acc_low[...] = acc[lower, :]
-        for s in HALVES:
-            total = acc_low if s == 0 else acc.at[lower]
-            for turn, k in enumerate((1 - near, 2, 3, near)):
-                own = pl.ds(pl.multiple_of(k * nodes, nodes), nodes)
-                with scope("wlat%d%d" % (s, turn)):
-                    lat_copy(outer, s, k, (p + 1) % lat_count).wait_recv()
-                gain(own, OMEGA * COUPLE * unpack(lat_in[outer, s, k], s), s)
-                round_u(own)
-                columns = own
-                if outer == 1:
-                    if turn < 3:
-                        continue
-                    columns = upper
-                for block in (slice(0, nodes), slice(nodes, 2 * nodes)):
-                    rows = slice(4 * nodes + block.start, 4 * nodes + block.stop)
-                    total[block, :] = total[block, :] + product(rows, columns)
-                if outer == 0 and s == 1 and turn == 0:
-                    relay(second_layer, first, 0)
-            with scope("sendlow%d" % s):
+        round_u(lower)
+        if outer < ITERS - 1:
+            with scope("lacc"):
+                for block in blocks(every):
+                    moved = product(block, lower)
+                    ahead[block, :] = moved
+                    behind[block, :] = moved
+            for s, acc in enumerate((ahead, behind)):
+                for turn, k in enumerate(order):
+                    own = arrive(outer, s, k)
+                    add(acc, lower, own)
+                    if s == 1 and turn == 0:
+                        relay(second_layer, first, 0)
+                with scope("sendlow%d" % s):
+                    send_low(first, s, lambda rows: acc[rows, :])
                 if s == 0:
-                    send_low(first, s, lambda rows: acc_low[rows.start - 4 * nodes : rows.stop - 4 * nodes, :])
-                else:
-                    send_low(first, s, lambda rows: acc[rows, :])
-        if outer == 0:
+                    with scope("bulkA"):
+                        bulk_rows(acc, s)
+                        begin(acc, every, upper)
             relay(later_layer, first, 0)
-        with scope("bulk1"):
-            add(upper, upper)
-            u[upper, :] = u[upper, :] + OMEGA * residual(upper)
-            round_u(upper)
-        if outer == 1:
-            relay(second_layer, first, 0)
-        with scope("bulk2"):
-            begin(upper)
-        relay(second_layer, first, 1)
-        if outer == 1:
-            relay(later_layer, first, 0)
-            relay(later_layer, first, 1)
-        for s in HALVES:
-            take(first, s)
-            apply_h(first, s)
-            apply_dn(first, s)
-            with scope("fin%d" % s):
-                round_half(lower, s)
-                if outer < ITERS - 1:
+            for s, acc in enumerate((ahead, behind)):
+                if s == 1:
+                    with scope("bulkB1"):
+                        bulk_rows(acc, s)
+                    relay(second_layer, first, 1)
+                    with scope("bulkB2"):
+                        begin(acc, every, upper)
+                    relay(later_layer, first, 1)
+                close(first, s, acc)
+                with scope("fin%d" % s):
+                    round_u(lower)
                     for block in blocks(upper):
-                        gain(block, OMEGA * left_over(block, added(block)), s)
-            with scope("sendlow2%d" % s):
-                sums = added(lower)
-                send_low(second, s, lambda rows: sums[rows.start - 4 * nodes : rows.stop - 4 * nodes, :])
-            if outer < ITERS - 1:
-                if s == 0:
-                    relay(later_layer, first, 1)
-                else:
+                        gain(block, OMEGA * left_over(block, acc[block, :] + product(block, lower)), s)
+                if s == 1:
+                    send_next(second, s, acc)
                     relay(second_layer, second, 0)
                 with scope("faces%d" % s):
                     send_faces(outer + 1, s)
-        if outer < ITERS - 1:
+                if s == 0:
+                    send_next(second, s, acc)
             relay(later_layer, second, 0)
             relay(inner_layer, second, 1)
             with scope("bulk3"):
                 round_u(upper)
-                begin(upper)
+                begin(behind, every, upper)
             for s in HALVES:
-                take(second, s)
-                apply_h(second, s)
-                apply_dn(second, s)
+                close(second, s, behind)
             with scope("bulk4"):
                 round_u(lower)
-                add(every, lower)
+                advance_all(behind)
+        else:
+            with scope("lacc"):
+                begin(behind, lower, lower)
+            for s in HALVES:
+                for k in order:
+                    arrive(outer, s, k)
+                acc = ahead if s == 0 else behind
+                for block in blocks(lower):
+                    acc[block, :] = behind[block, :] + product(block, upper)
+                with scope("sendlow%d" % s):
+                    send_low(first, s, lambda rows: acc[rows, :])
+            relay(second_layer, first, 0)
+            with scope("bulk1"):
+                for block in blocks(upper):
+                    total = product(block, every)
+                    u[block, :] = u[block, :] + OMEGA * left_over(block, total)
+                round_u(upper)
+            with scope("bulk2"):
+                begin(behind, lower, upper)
+            relay(later_layer, first, 0)
+            relay(inner_layer, first, 1)
+            for s in HALVES:
+                close(first, s, behind)
+                round_half(lower, s)
+                send_next(second, s, behind)
+                relay(second_layer, second, s)
     with scope("lastup"):
         for block in blocks(upper):
-            u[block, :] = u[block, :] + OMEGA * left_over(block, added(block))
+            u[block, :] = u[block, :] + OMEGA * left_over(block, product(block, every))
     final = ITERS * RADIAL_PASSES - 1
     stores = [
         pltpu.make_async_copy(u.at[part], out_hbm.at[0, 0, part], out_sem.at[n])
@@ -393,7 +420,7 @@
     ]
     stores[0].start()
     for s in HALVES:
-        relay(inner_layer, final, s)
+        relay(later_layer, final, s)
         take(final, s)
         apply_h(final, s)
     stores[1].start()
@@ -445,8 +472,7 @@
             wide(jnp.float32),
             faces(),
             wide(jnp.float32),
-            wide(jnp.float32),
-            pltpu.VMEM((2 * nodes, columns), jnp.float32),
+            pltpu.VMEM((2, order, columns), jnp.float32),
             packed(),
             packed(),
             pltpu.VMEM((4, nodes, nodes), jnp.bfloat16),

time: 41.3 us -> 40 us (0.969)
  Pallas kernels: 39.9 us -> 38.7 us
    pallas_call x1, Pallas kernels: 39.9 us -> 38.7 us  [per_device(): pl.pallas_call(functools.partial(kernel, lat_count, rad_count, nodes), ou...]
where the time goes in v5:
time: 40 us; the launch traced here: 39.6 us
  Pallas kernels  38.7 us (97%)
  local copies, waits for them, and re-layouts  0.88 us (2%)
    pallas_call x1, Pallas kernels, per_device(): pl.pallas_call(functools.partial(kernel, lat_count, rad_count, nodes), ou...  38.7 us
    unnamed x1, local copies, waits for them, and re-layouts  0.88 us

profile of v5, /device:TPU:24, one launch (start us, length us, event | category | flops | bytes accessed | tf_op | source)
XLA Modules:
  0.0 39.6 jit_solution(520661854217576263)
XLA Ops:
  0.0 38.7 %shell.1 = f32[1,1,1536,128]{3,2,1,0:T(8,128)S(1)} custom-call(s32[4,8]{1,0:T(4,128)} %bitcast.2, s32[4,8]{1,0:T(4,128)} %bitcast.3, f32[1,1,1536]{2,1,0:T(1,128)} %diag_hbm.1, bf16[1,1,1536,1536]{3,2,1,0:T(8,128)(2,1)} %w_hbm.1, f32[1,1,1536,128]{3,2,1,0:T(8,128)} %source_hbm.1, f32[1,1,1536,128]{3,2,1,0:T(8,128)} %start_hbm.1, f32[1,1,256,128]{3,2,1,0:T(8,128)} %decay_hbm.1), custom_call_target="tpu_custom_call" | custom-call | tf_op jit(solution)/shard_map/shell/pallas_call | solution.py:460
  38.7 0.9 %copy.9 = f32[1,1,1536,128]{3,2,1,0:T(8,128)} copy(f32[1,1,1536,128]{3,2,1,0:T(8,128)S(1)} %shell.1) | data formatting | bytes 1572864

commit v6 on v5

--- a/solution.py
+++ b/solution.py
@@ -130,31 +130,31 @@
     def lat_copy(outer, s, k, target):
         return pltpu.make_async_remote_copy(
             src_ref=lat_out.at[outer, s, k], dst_ref=lat_in.at[outer, s, k],
-            send_sem=lat_send.at[outer], recv_sem=lat_recv.at[outer, s, k],
+            send_sem=lat_send.at[0], recv_sem=lat_recv.at[outer, s, k],
             device_id={"lat": target}, device_id_type=MESH,
         )
 
     def lat_target(k):
         return (p - offsets[k] + lat_count) % lat_count
 
-    def lat_sent(outer):
+    def lat_sent():
         return pltpu.make_async_remote_copy(
-            src_ref=lat_out.at[outer], dst_ref=lat_in.at[outer],
-            send_sem=lat_send.at[outer], recv_sem=lat_recv.at[outer, 0, 0],
+            src_ref=lat_out, dst_ref=lat_in,
+            send_sem=lat_send.at[0], recv_sem=lat_recv.at[0, 0, 0],
             device_id={"lat": (p + 1) % lat_count}, device_id_type=MESH,
         )
 
     def dn_copy(sweep, s):
         return pltpu.make_async_remote_copy(
             src_ref=dn_out.at[sweep, s], dst_ref=dn_in.at[sweep, s],
-            send_sem=dn_send.at[sweep], recv_sem=dn_recv.at[sweep % 2, s],
+            send_sem=dn_send.at[0], recv_sem=dn_recv.at[sweep % 2, s],
             device_id={"rad": below}, device_id_type=MESH,
         )
 
-    def dn_sent(sweep):
+    def dn_sent():
         return pltpu.make_async_remote_copy(
-            src_ref=dn_out.at[sweep], dst_ref=dn_in.at[sweep],
-            send_sem=dn_send.at[sweep], recv_sem=dn_recv.at[sweep % 2, 0],
+            src_ref=dn_out, dst_ref=dn_in,
+            send_sem=dn_send.at[0], recv_sem=dn_recv.at[0, 0],
             device_id={"rad": below}, device_id_type=MESH,
         )
 
@@ -162,14 +162,14 @@
         rows = pl.ds(c * size, size)
         return pltpu.make_async_remote_copy(
             src_ref=h_out.at[sweep, s, rows], dst_ref=h_in.at[sweep, s, rows],
-            send_sem=h_send.at[sweep], recv_sem=h_recv.at[sweep % 2, s, c],
+            send_sem=h_send.at[0], recv_sem=h_recv.at[sweep % 2, s, c],
             device_id={"rad": above}, device_id_type=MESH,
         )
 
-    def h_sent(sweep):
+    def h_sent():
         return pltpu.make_async_remote_copy(
-            src_ref=h_out.at[sweep], dst_ref=h_in.at[sweep],
-            send_sem=h_send.at[sweep], recv_sem=h_recv.at[sweep % 2, 0, 0],
+            src_ref=h_out, dst_ref=h_in,
+            send_sem=h_send.at[0], recv_sem=h_recv.at[0, 0, 0],
             device_id={"rad": above}, device_id_type=MESH,
         )
 
@@ -363,13 +363,13 @@
                         begin(acc, every, upper)
                     relay(later_layer, first, 1)
                 close(first, s, acc)
-                with scope("fin%d" % s):
-                    round_u(lower)
-                    for block in blocks(upper):
-                        gain(block, OMEGA * left_over(block, acc[block, :] + product(block, lower)), s)
+                round_u(lower)
                 if s == 1:
                     send_next(second, s, acc)
                     relay(second_layer, second, 0)
+                with scope("fin%d" % s):
+                    for block in blocks(upper):
+                        gain(block, OMEGA * left_over(block, acc[block, :] + product(block, lower)), s)
                 with scope("faces%d" % s):
                     send_faces(outer + 1, s)
                 if s == 0:
@@ -409,14 +409,15 @@
                 close(first, s, behind)
                 round_half(lower, s)
                 send_next(second, s, behind)
+            for s in HALVES:
                 relay(second_layer, second, s)
     with scope("lastup"):
         for block in blocks(upper):
             u[block, :] = u[block, :] + OMEGA * left_over(block, product(block, every))
     final = ITERS * RADIAL_PASSES - 1
     stores = [
-        pltpu.make_async_copy(u.at[part], out_hbm.at[0, 0, part], out_sem.at[n])
-        for n, part in enumerate((upper, bottom, top))
+        pltpu.make_async_copy(u.at[part], out_hbm.at[0, 0, part], out_sem.at[0])
+        for part in (upper, bottom, top)
     ]
     stores[0].start()
     for s in HALVES:
@@ -429,22 +430,18 @@
     stores[2].start()
 
     with scope("wsend"):
-        for outer in range(ITERS):
-            lat_sent(outer).wait_send()
+        lat_sent().wait_send()
 
         @pl.when(r > 0)
         def _():
-            for sweep in range(ITERS * RADIAL_PASSES):
-                dn_sent(sweep).wait_send()
+            dn_sent().wait_send()
 
         @pl.when(r < rad_count - 1)
         def _():
-            for sweep in range(ITERS * RADIAL_PASSES):
-                h_sent(sweep).wait_send()
+            h_sent().wait_send()
 
     with scope("wout"):
-        for copy in stores:
-            copy.wait()
+        pltpu.make_async_copy(u, out_hbm.at[0, 0], out_sem.at[0]).wait()
 
 
 def per_device(lat_count, rad_count, schur_off, schur_diag, source, start, decay, neighbour_face, orientation):
@@ -479,9 +476,9 @@
             pltpu.VMEM((ITERS, 2, 4, nodes // 2, columns), jnp.float32),
             pltpu.VMEM((ITERS, 2, 4, nodes // 2, columns), jnp.float32),
             packed(sweeps), packed(sweeps), packed(sweeps), packed(sweeps),
-            dma(3), dma(3), dma(2), dma(3),
-            dma(ITERS), dma(ITERS, 2, 4), dma(sweeps), dma(2, 2),
-            dma(sweeps), dma(2, 2, CHUNKS),
+            dma(3), dma(3), dma(2), dma(1),
+            dma(1), dma(ITERS, 2, 4), dma(1), dma(2, 2),
+            dma(1), dma(2, 2, CHUNKS),
         ],
         compiler_params=pltpu.CompilerParams(
             collective_id=0, has_side_effects=True, vmem_limit_bytes=24 * 1024 * 1024

time: 40 us -> 39.3 us (0.982)
  Pallas kernels: 38.7 us -> 38.2 us
    pallas_call x1, Pallas kernels: 38.7 us -> 38.2 us  [per_device(): pl.pallas_call(functools.partial(kernel, lat_count, rad_count, nodes), ou...]
where the time goes in v6:
time: 39.3 us; the launch traced here: 39.1 us
  Pallas kernels  38.2 us (97%)
  local copies, waits for them, and re-layouts  0.88 us (2%)
    pallas_call x1, Pallas kernels, per_device(): pl.pallas_call(functools.partial(kernel, lat_count, rad_count, nodes), ou...  38.2 us
    unnamed x1, local copies, waits for them, and re-layouts  0.88 us

profile of v6, /device:TPU:24, one launch (start us, length us, event | category | flops | bytes accessed | tf_op | source)
XLA Modules:
  0.0 39.1 jit_solution(3554467838668129651)
XLA Ops:
  0.0 38.2 %shell.1 = f32[1,1,1536,128]{3,2,1,0:T(8,128)S(1)} custom-call(s32[4,8]{1,0:T(4,128)} %bitcast.2, s32[4,8]{1,0:T(4,128)} %bitcast.3, f32[1,1,1536]{2,1,0:T(1,128)} %diag_hbm.1, bf16[1,1,1536,1536]{3,2,1,0:T(8,128)(2,1)} %w_hbm.1, f32[1,1,1536,128]{3,2,1,0:T(8,128)} %source_hbm.1, f32[1,1,1536,128]{3,2,1,0:T(8,128)} %start_hbm.1, f32[1,1,256,128]{3,2,1,0:T(8,128)} %decay_hbm.1), custom_call_target="tpu_custom_call" | custom-call | tf_op jit(solution)/shard_map/shell/pallas_call | solution.py:457
  38.2 0.9 %copy.9 = f32[1,1,1536,128]{3,2,1,0:T(8,128)} copy(f32[1,1,1536,128]{3,2,1,0:T(8,128)S(1)} %shell.1) | data formatting | bytes 1572864

commit v7 on v6

--- a/solution.py
+++ b/solution.py
@@ -15,7 +15,6 @@
 COUPLE = 0.5
 CHUNKS = 8
 HALVES = (0, 1)
-SEND_ORDER = (2, 3, 0, 1)
 MESH = pl.DeviceIdType.MESH
 
 
@@ -135,7 +134,8 @@
         )
 
     def lat_target(k):
-        return (p - offsets[k] + lat_count) % lat_count
+        reach = 1 + (k // 2) * (far - 1)
+        return (p - (2 * (k % 2) - 1) * reach + lat_count) % lat_count
 
     def lat_sent():
         return pltpu.make_async_remote_copy(
@@ -173,6 +173,10 @@
             device_id={"rad": above}, device_id_type=MESH,
         )
 
+    near, pair = lax.rem(p, 2), lax.rem(p // 2, 2)
+    send_order = (2 + pair, 3 - pair, 1 - near, near)
+    order = (1 - near, 3 - pair, 2 + pair, near)
+
     def make_hot(k):
         hot[k] = one_hot(code_at[k, lat_target(k)], side)
 
@@ -184,11 +188,11 @@
         return permuted(hot[k], face)
 
     def send_faces(outer, s):
-        for pair in (SEND_ORDER[:2], SEND_ORDER[2:]):
-            faces = [pack(oriented(k), s) for k in pair]
-            for k, face in zip(pair, faces):
+        for some in (send_order[:2], send_order[2:]):
+            faces = [pack(oriented(k), s) for k in some]
+            for k, face in zip(some, faces):
                 lat_out[outer, s, k] = face
-            for k in pair:
+            for k in some:
                 lat_copy(outer, s, k, lat_target(k)).start()
 
     def product(rows, columns):
@@ -285,10 +289,12 @@
             low = acc[lower, :] + product(lower, lower)
             send_low(sweep, s, lambda rows: low[rows.start - 4 * nodes : rows.stop - 4 * nodes, :])
 
-    def advance_all(acc):
+    def advance_half(acc, s):
+        round_half(lower, s)
         for block in blocks(every):
             total = acc[block, :] + product(block, lower)
-            u[block, :] = u[block, :] + OMEGA * left_over(block, total)
+            gain(block, OMEGA * left_over(block, total), s)
+        round_half(lower, s)
 
     def bulk_rows(acc, s):
         add(acc, upper, upper)
@@ -298,20 +304,20 @@
 
     load_face.wait()
     load_code.wait()
-    for k in SEND_ORDER:
+    for k in range(len(offsets)):
         make_hot(k)
     with scope("loadu"):
         load_u.wait()
     with scope("mkf"):
-        for k in SEND_ORDER:
+        for n, k in enumerate(send_order):
             face = oriented(k)
             for s in HALVES:
                 lat_out[0, s, k] = pack(face, s)
-            if k == SEND_ORDER[0]:
+            if n == 0:
                 with scope("bar"):
                     pl.semaphore_wait(barrier, len(offsets) + inner)
             lat_copy(0, 0, k, lat_target(k)).start()
-        for k in SEND_ORDER:
+        for k in send_order:
             lat_copy(0, 1, k, lat_target(k)).start()
     round_u(every)
     load_diag.wait()
@@ -330,12 +336,10 @@
         for block in blocks(every):
             u[block, :] = u[block, :] + OMEGA * left_over(block, product(block, every))
 
-    near = lax.rem(p, 2)
-    order = (1 - near, 2, 3, near)
     for outer in range(ITERS):
         first, second = outer * RADIAL_PASSES, outer * RADIAL_PASSES + 1
-        round_u(lower)
         if outer < ITERS - 1:
+            round_u(lower)
             with scope("lacc"):
                 for block in blocks(every):
                     moved = product(block, lower)
@@ -379,20 +383,17 @@
             with scope("bulk3"):
                 round_u(upper)
                 begin(behind, every, upper)
+        else:
             for s in HALVES:
-                close(second, s, behind)
-            with scope("bulk4"):
-                round_u(lower)
-                advance_all(behind)
-        else:
-            with scope("lacc"):
-                begin(behind, lower, lower)
-            for s in HALVES:
+                close(first - 1, s, behind)
+                with scope("bulk4"):
+                    advance_half(behind, s)
+                acc = ahead
+                with scope("lacc"):
+                    begin(acc, lower, lower)
                 for k in order:
                     arrive(outer, s, k)
-                acc = ahead if s == 0 else behind
-                for block in blocks(lower):
-                    acc[block, :] = behind[block, :] + product(block, upper)
+                add(acc, lower, upper)
                 with scope("sendlow%d" % s):
                     send_low(first, s, lambda rows: acc[rows, :])
             relay(second_layer, first, 0)

time: 39.3 us -> 39 us (level)
  no operation moved by 1% of the time
where the time goes in v7:
time: 39 us; the launch traced here: 38.8 us
  Pallas kernels  37.9 us (97%)
  local copies, waits for them, and re-layouts  0.88 us (2%)
    pallas_call x1, Pallas kernels, per_device(): pl.pallas_call(functools.partial(kernel, lat_count, rad_count, nodes), ou...  37.9 us
    unnamed x1, local copies, waits for them, and re-layouts  0.88 us

profile of v7, /device:TPU:24, one launch (start us, length us, event | category | flops | bytes accessed | tf_op | source)
XLA Modules:
  0.0 38.8 jit_solution(1801580302777153520)
XLA Ops:
  0.0 37.9 %shell.1 = f32[1,1,1536,128]{3,2,1,0:T(8,128)S(1)} custom-call(s32[4,8]{1,0:T(4,128)} %bitcast.2, s32[4,8]{1,0:T(4,128)} %bitcast.3, f32[1,1,1536]{2,1,0:T(1,128)} %diag_hbm.1, bf16[1,1,1536,1536]{3,2,1,0:T(8,128)(2,1)} %w_hbm.1, f32[1,1,1536,128]{3,2,1,0:T(8,128)} %source_hbm.1, f32[1,1,1536,128]{3,2,1,0:T(8,128)} %start_hbm.1, f32[1,1,256,128]{3,2,1,0:T(8,128)} %decay_hbm.1), custom_call_target="tpu_custom_call" | custom-call | tf_op jit(solution)/shard_map/shell/pallas_call | solution.py:458
  37.9 0.9 %copy.9 = f32[1,1,1536,128]{3,2,1,0:T(8,128)} copy(f32[1,1,1536,128]{3,2,1,0:T(8,128)S(1)} %shell.1) | data formatting | bytes 1572864
